TPU v7x, 32 devices: a whole 2x2x4 slice. The times are simulated.
32 devices in a mesh: section: 2 (over y), pen: 8 (over z, x), slab: 2 (over core).
Axes of the slice: x: 2, y: 2, z: 4, core: 2. Of those that a mesh axis runs over, the one named last changes fastest.
Arguments:
- velocity: float32 [3, 48, 48, 48], P(None, ('section', 'pen'), 'slab'), may hold values from -6 to 6
- vorticity: float32 [3, 48, 48, 48], P(None, ('section', 'pen'), 'slab'), may hold values from -6 to 6
- velocity_modes: float32 [3, 32, 32, 2, 32], P(None, None, ('section', 'pen'), None, 'slab'), may hold values from -6 to 6
Outputs:
- rhs_modes: float32 [3, 32, 32, 2, 32], P(None, None, ('section', 'pen'), None, 'slab')
All inputs are finite; a program needn't handle non-finite values.
Results may differ from a plain program's by a relative error of at most 0.000057.
Values sent between devices are 32-bit elements; how exact they have to be, the bound alone decides.
A program may use at most 64 MiB of HBM per device.

v0:
```python
import math

import jax
import jax.numpy as jnp
from jax import lax
from jax.sharding import PartitionSpec as P

highest = lax.Precision.HIGHEST


def signed_modes(index, count):
    return jnp.where(index < count // 2, index, index - count)


def discrete_fourier_tables(length, keep_count):
    modes = signed_modes(jnp.arange(keep_count, dtype=jnp.int32), keep_count)
    mode_positions = jnp.arange(length, dtype=jnp.int32)
    phase = jnp.remainder(modes[:, None] * mode_positions[None, :], length).astype(jnp.float32)
    angles = 2.0 * math.pi / length * phase
    factor = 1.0 / math.sqrt(length)
    return (jnp.cos(angles) * factor, jnp.sin(angles) * factor)


def complex_apply(form, cosine, sine, real_part, imag_part):
    out_real = jnp.einsum(form, cosine, real_part, precision=highest) + jnp.einsum(
        form, sine, imag_part, precision=highest
    )
    out_imag = jnp.einsum(form, cosine, imag_part, precision=highest) - jnp.einsum(
        form, sine, real_part, precision=highest
    )
    return (out_real, out_imag)


def per_device(velocity, vorticity, velocity_modes):
    grid_cells = velocity.shape[3]
    keep_count = velocity_modes.shape[1]
    cross_product = jnp.stack(
        [
            velocity[1] * vorticity[2] - velocity[2] * vorticity[1],
            velocity[2] * vorticity[0] - velocity[0] * vorticity[2],
            velocity[0] * vorticity[1] - velocity[1] * vorticity[0],
        ]
    )
    slabs = lax.axis_size("slab")
    block_modes = keep_count // slabs
    cosine_table, sine_table = discrete_fourier_tables(grid_cells, keep_count)
    cols_real = cosine_table.T.reshape(grid_cells, slabs, block_modes)
    cols_imag = (-sine_table).T.reshape(grid_cells, slabs, block_modes)
    column_table = jnp.stack([cols_real, cols_imag], axis=2).reshape(grid_cells, 2 * keep_count)
    first_pass = jnp.einsum("czyx,xj->czyj", cross_product, column_table, precision=highest)
    block = lax.all_to_all(first_pass, "slab", split_axis=3, concat_axis=2, tiled=True)
    out_real, out_imag = complex_apply(
        "ky,czyj->czkj",
        cosine_table,
        sine_table,
        block[..., :block_modes],
        block[..., block_modes:],
    )
    second_pass = jnp.concatenate([out_real, out_imag], axis=-1)
    halves = lax.axis_size("section")
    pens = lax.axis_size("pen")
    rows_ky = keep_count // (halves * pens)
    block = lax.all_to_all(second_pass, ("section", "pen"), split_axis=2, concat_axis=1, tiled=True)
    out_real, out_imag = complex_apply(
        "kz,czyj->ckyj",
        cosine_table,
        sine_table,
        block[..., :block_modes],
        block[..., block_modes:],
    )
    third_pass = jnp.concatenate([out_real, out_imag], axis=-1)
    group_index = lax.axis_index("section") * pens + lax.axis_index("pen")
    modes_z = signed_modes(jnp.arange(keep_count, dtype=jnp.int32), keep_count)[:, None, None]
    modes_y = signed_modes(
        group_index * rows_ky + jnp.arange(rows_ky, dtype=jnp.int32), keep_count
    )[None, :, None]
    modes_x = signed_modes(
        lax.axis_index("slab") * block_modes + jnp.arange(block_modes, dtype=jnp.int32), keep_count
    )[None, None, :]
    limit = -(keep_count // 2)
    keep_mask = ((modes_x != limit) & (modes_y != limit) & (modes_z != limit)).astype(jnp.float32)
    waves = (modes_x.astype(jnp.float32), modes_y.astype(jnp.float32), modes_z.astype(jnp.float32))
    ksq = waves[0] * waves[0] + waves[1] * waves[1] + waves[2] * waves[2]
    denom = jnp.maximum(ksq, 1.0)
    parts = []
    for which in range(2):
        chosen = third_pass[..., which * block_modes : (which + 1) * block_modes]
        comp = [chosen[c] for c in range(3)]
        inner = (waves[0] * comp[0] + waves[1] * comp[1] + waves[2] * comp[2]) / denom
        parts.append(jnp.stack([comp[c] - waves[c] * inner for c in range(3)]))
    projected = jnp.stack(parts, axis=3)
    visc = 0.5 / (keep_count // 2) ** 2
    return (
        projected * keep_mask[None, :, :, None, :]
        - visc * ksq[None, :, :, None, :] * velocity_modes
    )


def solution(mesh):
    return jax.shard_map(
        per_device,
        mesh=mesh,
        in_specs=(
            P(None, ("section", "pen"), "slab", None),
            P(None, ("section", "pen"), "slab", None),
            P(None, None, ("section", "pen"), None, "slab"),
        ),
        out_specs=P(None, None, ("section", "pen"), None, "slab"),
        check_vma=False,
    )
```

profile of v0, /device:TPU:0, one launch (start us, length us, event | category | flops | bytes accessed | tf_op | source)
XLA Modules:
  0.0 32.4 jit_solution(18080253306396795170)
XLA Ops:
  0.0 0.2 cosine_multiply_fusion.1
  0.2 0.9 %multiply_subtract_fusion.2 = (f32[1,3,24,48]{3,2,1,0:T(8,128)S(1)}, f32[1,3,24,48]{3,2,1,0:T(8,128)S(1)}, f32[1,3,24,48]{3,2,1,0:T(8,128)S(1)}) fusion(f32[3,3,24,48]{3,2,1,0:T(8,128)} %param.4, f32[3,3,24,48]{3,2,1,0:T(8,128)} %param.3), kind=kLoop, calls=%fused_computation.28 | loop fusion | flops 31104 | bytes 124416 | tf_op jit(solution)/shard_map/sub | solution.py:39
  1.1 0.3 %fusion.10 = f32[3,3,24,64]{3,2,1,0:T(8,128)S(1)} fusion(f32[48,64,1,1]{0,1,3,2:T(8,128)S(1)} %bitcast.64, f32[1,3,24,48]{3,2,1,0:T(8,128)S(1)} %get-tuple-element.10, f32[1,3,24,48]{3,2,1,0:T(8,128)S(1)} %get-tuple-element.11, f32[1,3,24,48]{3,2,1,0:T(8,128)S(1)} %get-tuple-element.9), kind=kOutput, calls=%fused_computation.15 | convolution fusion | flops 7983360 | bytes 109056 | tf_op jit(solution)/shard_map/czyx,xj->czyj/dot_general | solution.py:50
  1.4 0.2 copy.19
  1.6 0.9 %reshape.210 = f32[2,1,6912]{2,1,0:T(1,128)} reshape(f32[64,3,3,24]{3,2,1,0:T(4,128)S(1)} %bitcast.59) | data formatting | bytes 110592
  2.6 3.3 %all-to-all-start = ((f32[2,1,6912]{2,1,0:T(1,128)}), f32[2,1,6912]{2,1,0:T(1,128)S(1)}, u32[]{:S(2)}, u32[]{:S(2)}) async-start(f32[2,1,6912]{2,1,0:T(1,128)} %reshape.210), calls=%async_computation | async-start | bytes 110592 | tf_op jit(solution)/shard_map/all_to_all | solution.py:51
  5.9 1.4 %all-to-all-done = f32[2,1,6912]{2,1,0:T(1,128)S(1)} async-done(((f32[2,1,6912]{2,1,0:T(1,128)}), f32[2,1,6912]{2,1,0:T(1,128)S(1)}, u32[]{:S(2)}, u32[]{:S(2)}) %all-to-all-start) | async-done | bytes 55328 | tf_op jit(solution)/shard_map/all_to_all | solution.py:51
  7.2 0.5 %broadcast.464 = f32[]{:T(128)} broadcast(f32[]{:T(128)} %constant.195), dimensions={} | broadcast | bytes 8 | tf_op jit(solution)/shard_map/all_to_all | solution.py:51
  7.7 0.7 %reduce = f32[2,6912]{1,0:T(2,128)S(1)} reduce(f32[2,1,6912]{2,1,0:T(1,128)S(1)} %all-to-all-done, f32[]{:T(128)} %broadcast.464), dimensions={1}, to_apply=%all_to_all.26.reduce_sub_computation | reduce | bytes 110596 | tf_op jit(solution)/shard_map/all_to_all | solution.py:51
  8.5 0.3 reshape.211
  8.8 0.2 copy.20
  8.9 0.5 %fusion.7 = f32[3,3,16,32]{3,2,1,0:T(8,128)S(1)} fusion(f32[3,3,48,32]{3,2,1,0:T(8,128)S(1)} %bitcast.54, s32[32]{0:T(128)S(1)} %compare_select_fusion.3), kind=kOutput, calls=%fused_computation.11 | convolution fusion | flops 2669568 | bytes 73856 | tf_op jit(solution)/shard_map/ky,czyj->czkj/dot_general | solution.py:25
  9.5 0.6 %fusion.5 = f32[3,3,16,32]{3,2,1,0:T(8,128)S(1)} fusion(f32[3,3,48,32]{3,2,1,0:T(8,128)S(1)} %bitcast.55, s32[32]{0:T(128)S(1)} %compare_select_fusion.3), kind=kOutput, calls=%fused_computation.9 | convolution fusion | flops 2669568 | bytes 73856 | tf_op jit(solution)/shard_map/ky,czyj->czkj/dot_general | solution.py:28
  10.1 0.6 %fusion.1 = f32[3,3,32,16]{2,3,1,0:T(8,128)S(1)} fusion(f32[3,3,16,32]{3,2,1,0:T(8,128)S(1)} %fusion.7, f32[3,3,48,32]{3,2,1,0:T(8,128)S(1)} %bitcast.56, s32[32]{0:T(128)S(1)} %compare_select_fusion.3), kind=kOutput, calls=%fused_computation.3 | convolution fusion | flops 2674176 | bytes 92288 | tf_op jit(solution)/shard_map/ky,czyj->czkj/dot_general | solution.py:25
  10.7 0.5 %fusion = f32[3,3,32,16]{2,3,1,0:T(8,128)S(1)} fusion(f32[3,3,16,32]{3,2,1,0:T(8,128)S(1)} %fusion.5, f32[3,3,48,32]{3,2,1,0:T(8,128)S(1)} %bitcast.57, s32[32]{0:T(128)S(1)} %compare_select_fusion.3), kind=kOutput, calls=%fused_computation.1 | convolution fusion | flops 2674176 | bytes 92288 | tf_op jit(solution)/shard_map/ky,czyj->czkj/dot_general | solution.py:28
  11.3 0.1 copy.23
  11.4 0.8 %reshape.212 = f32[16,1,576]{2,1,0:T(1,128)} reshape(f32[32,3,3,32]{3,2,1,0:T(4,128)S(1)} %bitcast.61) | data formatting | bytes 73728
  12.2 8.3 %all-to-all-start.1 = ((f32[16,1,576]{2,1,0:T(1,128)}), f32[16,1,576]{2,1,0:T(1,128)S(1)}, u32[]{:S(2)}, u32[]{:S(2)}) async-start(f32[16,1,576]{2,1,0:T(1,128)} %reshape.212), calls=%async_computation.1 | async-start | bytes 81920 | tf_op jit(solution)/shard_map/all_to_all | solution.py:63
  21.0 7.0 %all-to-all-done.1 = f32[16,1,576]{2,1,0:T(1,128)S(1)} async-done(((f32[16,1,576]{2,1,0:T(1,128)}), f32[16,1,576]{2,1,0:T(1,128)S(1)}, u32[]{:S(2)}, u32[]{:S(2)}) %all-to-all-start.1) | async-done | bytes 36896 | tf_op jit(solution)/shard_map/all_to_all | solution.py:63
  28.0 0.7 %reduce.1 = f32[16,576]{1,0:T(8,128)S(1)} reduce(f32[16,1,576]{2,1,0:T(1,128)S(1)} %all-to-all-done.1, f32[]{:T(128)} %broadcast.464), dimensions={1}, to_apply=%all_to_all.30.reduce_sub_computation | reduce | bytes 73732 | tf_op jit(solution)/shard_map/all_to_all | solution.py:63
  28.6 0.1 reshape.213
  28.9 0.2 fusion.118
  29.1 0.1 copy.37
  29.2 0.3 %fusion.25 = f32[3,2,16,32]{3,2,1,0:T(8,128)S(1)} fusion(f32[3,48,2,16]{1,3,2,0:T(8,128)S(1)} %copy.37, s32[32]{0:T(128)S(1)} %compare_select_fusion.3), kind=kOutput, calls=%fused_computation.40 | convolution fusion | flops 1784832 | bytes 30848 | tf_op jit(solution)/shard_map/kz,czyj->ckyj/dot_general | solution.py:28
  29.5 0.1 copy.36
  29.6 0.3 %fusion.27 = f32[3,2,16,32]{3,2,1,0:T(8,128)S(1)} fusion(f32[3,48,2,16]{1,3,2,0:T(8,128)S(1)} %copy.36, s32[32]{0:T(128)S(1)} %compare_select_fusion.3), kind=kOutput, calls=%fused_computation.42 | convolution fusion | flops 1784832 | bytes 30848 | tf_op jit(solution)/shard_map/kz,czyj->ckyj/dot_general | solution.py:25
  30.0 0.3 %fusion.2 = f32[3,32,2,16]{1,3,2,0:T(8,128)S(1)} fusion(f32[3,2,16,32]{3,2,1,0:T(8,128)S(1)} %fusion.25, f32[3,48,2,16]{1,3,2,0:T(8,128)S(1)} %copy.36, s32[32]{0:T(128)S(1)} %compare_select_fusion.3), kind=kOutput, calls=%fused_computation.5 | convolution fusion | flops 1787904 | bytes 43136 | tf_op jit(solution)/shard_map/kz,czyj->ckyj/dot_general | solution.py:28
  30.3 0.3 %fusion.3 = f32[3,32,2,16]{1,3,2,0:T(8,128)S(1)} fusion(f32[3,2,16,32]{3,2,1,0:T(8,128)S(1)} %fusion.27, f32[3,48,2,16]{1,3,2,0:T(8,128)S(1)} %copy.37, s32[32]{0:T(128)S(1)} %compare_select_fusion.3), kind=kOutput, calls=%fused_computation.7 | convolution fusion | flops 1787904 | bytes 43136 | tf_op jit(solution)/shard_map/kz,czyj->ckyj/dot_general | solution.py:25
  30.6 0.1 multiply_subtract_fusion.8
  30.7 0.1 multiply_subtract_fusion.4
  30.8 0.9 %copy-done = f32[3,32,2,2,16]{1,4,3,2,0:T(8,128)S(1)} copy-done((f32[3,32,2,2,16]{1,4,3,2,0:T(8,128)S(1)}, f32[3,32,2,2,16]{1,4,3,2,0:T(8,128)}, u32[]{:S(2)}) %copy-start) | copy-done | bytes 24600
  31.7 0.6 %copy.29 = f32[3,32,2,2,16]{1,4,3,2,0:T(8,128)} copy(f32[3,32,2,2,16]{1,4,2,0,3:T(8,128)S(1)} %fusion.16) | data formatting | bytes 49152 | tf_op jit(solution)/shard_map/sub | solution.py:94
  (22 shorter events, 0.5 us)
Async XLA Ops:
  2.6 4.7 %all-to-all-start = ((f32[2,1,6912]{2,1,0:T(1,128)}), f32[2,1,6912]{2,1,0:T(1,128)S(1)}, u32[]{:S(2)}, u32[]{:S(2)}) async-start(f32[2,1,6912]{2,1,0:T(1,128)} %reshape.210), calls=%async_computation | async-start | bytes 110592 | tf_op jit(solution)/shard_map/all_to_all | solution.py:51
  12.2 15.8 %all-to-all-start.1 = ((f32[16,1,576]{2,1,0:T(1,128)}), f32[16,1,576]{2,1,0:T(1,128)S(1)}, u32[]{:S(2)}, u32[]{:S(2)}) async-start(f32[16,1,576]{2,1,0:T(1,128)} %reshape.212), calls=%async_computation.1 | async-start | bytes 81920 | tf_op jit(solution)/shard_map/all_to_all | solution.py:63
  30.8 0.9 %copy-start = (f32[3,32,2,2,16]{1,4,3,2,0:T(8,128)S(1)}, f32[3,32,2,2,16]{1,4,3,2,0:T(8,128)}, u32[]{:S(2)}) copy-start(f32[3,32,2,2,16]{1,4,3,2,0:T(8,128)} %param.5) | copy-start | bytes 73732
where the time goes:
time: 32.7 us; the launch traced here: 32.4 us
  starting transfers between devices  11.6 us (35%)
  waiting for transfers between devices  8.39 us (26%)
  local copies, waits for them, and re-layouts  5.12 us (16%)
  matrix products  4 us (12%)
  other arithmetic  3 us (9%)
    all_to_all x1, starting transfers between devices, per_device(): lax.all_to_all(second_pass, ('section', 'pen'), split_axis=2, concat_axis...  8.34 us
    all_to_all x1, waiting for transfers between devices, per_device(): lax.all_to_all(second_pass, ('section', 'pen'), split_axis=2, concat_axis...  7.01 us
    all_to_all x1, starting transfers between devices, per_device(): lax.all_to_all(first_pass, 'slab', split_axis=3, concat_axis=2, tiled=True)  3.28 us
    unnamed x8, local copies, waits for them, and re-layouts  3.2 us
    all_to_all x1, waiting for transfers between devices, per_device(): lax.all_to_all(first_pass, 'slab', split_axis=3, concat_axis=2, tiled=True)  1.38 us
    dot_general x2, matrix products, complex_apply(): jnp.einsum(form, cosine, imag_part, precision=highest)  0.96 us
    dot_general x2, matrix products, complex_apply(): jnp.einsum(form, sine, imag_part, precision=highest)  0.95 us
    dot_general x2, matrix products, complex_apply(): jnp.einsum(form, cosine, real_part, precision=highest)  0.89 us
  transfers between devices with their start and end apart: 2, of which 2 were waited for; matrix products, arithmetic and copies ran while one was open for 1% of the time, Pallas kernels for 0%

commit v1 on v0

--- a/solution.py
+++ b/solution.py
@@ -1,10 +1,15 @@
+import functools
 import math
 
 import jax
 import jax.numpy as jnp
+import numpy as np
 from jax import lax
+from jax.experimental import pallas as pl
+from jax.experimental.pallas import tpu as pltpu
 from jax.sharding import PartitionSpec as P
 
+AXES = ("section", "pen", "slab")
 highest = lax.Precision.HIGHEST
 
 
@@ -96,9 +101,298 @@
     )
 
 
+def split_bf16(table):
+    high = table.astype(jnp.bfloat16)
+    low = (table - high.astype(np.float32)).astype(jnp.bfloat16)
+    return high, low
+
+
+def split_in_kernel(value):
+    high = value.astype(jnp.bfloat16)
+    low = (value - high.astype(jnp.float32)).astype(jnp.bfloat16)
+    return high, low
+
+
+def mm(a, b):
+    return lax.dot_general(a, b, (((1,), (0,)), ((), ())), preferred_element_type=jnp.float32)
+
+
+def split_dot(a, b):
+    return mm(a[0], b[0]) + mm(a[1], b[0]) + mm(a[0], b[1])
+
+
+def wave_numbers(count):
+    index = np.arange(count)
+    return np.where(index < count // 2, index, index - count)
+
+
+def host_tables(cells, keep):
+    phase = np.remainder(wave_numbers(keep)[:, None] * np.arange(cells)[None, :], cells)
+    angles = 2.0 * np.pi / cells * phase
+    factor = 1.0 / np.sqrt(cells)
+    return np.cos(angles) * factor, np.sin(angles) * factor
+
+
+class Plan:
+    def __init__(self, mesh_shape, cells, keep, z_rows, y_rows):
+        self.cells, self.keep, self.z_rows, self.y_rows = cells, keep, z_rows, y_rows
+        self.halves, self.pens, self.slabs = (mesh_shape[a] for a in AXES)
+        self.groups = self.halves * self.pens
+        self.count = self.groups * self.slabs
+        self.rows_ky = keep // self.groups
+        self.block = keep // self.slabs
+        self.field = self.rows_ky * 2 * self.block
+        self.rows = z_rows + (z_rows + 1) // 2
+        self.slots = 2 * self.rows_ky
+
+    def fits(self):
+        return (
+            2 * self.field == 128
+            and self.rows <= 8
+            and (self.rows * self.groups) % 16 == 0
+            and self.y_rows % 8 == 0
+            and self.keep % 8 == 0
+            and self.block % 8 == 0
+            and 3 * self.z_rows * self.y_rows <= 512
+            and self.count <= 64
+        )
+
+    def place(self, comp, z):
+        if comp < 2:
+            return z, comp
+        return self.z_rows + z // 2, z % 2
+
+    def tables(self):
+        cos, sin = host_tables(self.cells, self.keep)
+        g, zl, yl, ky_n, bm = self.groups, self.z_rows, self.y_rows, self.rows_ky, self.block
+        first = np.zeros((self.slabs, self.slots, 2, self.rows, g, 3, zl, yl), np.float32)
+        for c in range(3):
+            for z in range(zl):
+                row, half = self.place(c, z)
+                for ky in range(ky_n):
+                    for s in range(self.slabs):
+                        cells = slice(s * yl, (s + 1) * yl)
+                        first[s, half * ky_n + ky, 0, row, :, c, z] = cos[ky::ky_n, cells]
+                        first[s, half * ky_n + ky, 1, row, :, c, z] = -sin[ky::ky_n, cells]
+        first = first.reshape(self.slabs, self.slots * 2 * self.rows * g, 3 * zl * yl)
+        second = np.zeros((self.slots, 2, self.cells, self.slabs, self.slots, 2, bm), np.float32)
+        for s in range(self.slabs):
+            c_t = cos[s * bm : (s + 1) * bm].T
+            s_t = sin[s * bm : (s + 1) * bm].T
+            for q in range(self.slots):
+                second[q, 0, :, s, q, 0] = c_t
+                second[q, 0, :, s, q, 1] = -s_t
+                second[q, 1, :, s, q, 0] = s_t
+                second[q, 1, :, s, q, 1] = c_t
+        second = second.reshape(self.slots * 2, self.cells, self.slabs * 128)
+        third = np.zeros((3, 2, self.keep, g, self.slabs, 8), np.float32)
+        for z in range(zl):
+            for which, table in enumerate((cos, sin)):
+                column = table[:, z::zl][:, :, None]
+                third[0, which, :, :, :, z] = column
+                third[1 + z % 2, which, :, :, :, zl + z // 2] = column
+        third = third.reshape(6 * self.keep, self.count * 8)
+        return (
+            np.stack(split_bf16(first), axis=1),
+            np.stack(split_bf16(second)),
+            np.stack(split_bf16(third)),
+        )
+
+
+def kernel(
+    plan, vel_hbm, vort_hbm, modes_hbm, first_hbm, second_hbm, third_hbm, out_ref,
+    vel, vort, modes, first, second, third, send, recv, load_sem, send_sem, recv_sem,
+):
+    sec, pen, slab = (lax.axis_index(a) for a in AXES)
+    group = sec * plan.pens + pen
+    me = group * plan.slabs + slab
+    loads = [
+        pltpu.make_async_copy(src, dst, load_sem.at[i])
+        for i, (src, dst) in enumerate(
+            (
+                (vel_hbm, vel),
+                (vort_hbm, vort),
+                (first_hbm.at[slab], first),
+                (second_hbm, second),
+                (third_hbm, third),
+                (modes_hbm, modes),
+            )
+        )
+    ]
+    for load in loads:
+        load.start()
+
+    def spread(offset):
+        a, b, c = offset
+        to = (
+            lax.rem(sec + a, plan.halves),
+            lax.rem(pen + b, plan.pens),
+            lax.rem(slab + c, plan.slabs),
+        )
+        back = (
+            lax.rem(sec + plan.halves - a, plan.halves),
+            lax.rem(pen + plan.pens - b, plan.pens),
+            lax.rem(slab + plan.slabs - c, plan.slabs),
+        )
+        return to, (back[0] * plan.pens + back[1]) * plan.slabs + back[2]
+
+    offsets = [
+        (a, b, c)
+        for b in sorted(range(plan.pens), key=lambda v: -min(v, plan.pens - v))
+        for a in reversed(range(plan.halves))
+        for c in reversed(range(plan.slabs))
+    ]
+    offsets.remove((0, 0, 0))
+    recv[...] = jnp.zeros_like(recv)
+    barrier = pltpu.get_barrier_semaphore()
+    for offset in offsets:
+        pl.semaphore_signal(
+            barrier, inc=1, device_id=spread(offset)[0], device_id_type=pl.DeviceIdType.MESH
+        )
+
+    loads[0].wait()
+    loads[1].wait()
+    zl, yl, cells = plan.z_rows, plan.y_rows, plan.cells
+    v = [vel[c].reshape(zl * yl, cells) for c in range(3)]
+    w = [vort[c].reshape(zl * yl, cells) for c in range(3)]
+    cross = jnp.concatenate(
+        [v[1] * w[2] - v[2] * w[1], v[2] * w[0] - v[0] * w[2], v[0] * w[1] - v[1] * w[0]], axis=0
+    )
+    cross = split_in_kernel(cross)
+    loads[2].wait()
+    part = split_dot((first[0], first[1]), cross)
+    part = split_in_kernel(part)
+    loads[3].wait()
+    size = plan.rows * plan.groups
+    total = None
+    for i in range(2 * plan.slots):
+        piece = tuple(p[i * size : (i + 1) * size] for p in part)
+        term = split_dot(piece, (second[0, i], second[1, i]))
+        total = term if total is None else total + term
+    for s in range(plan.slabs):
+        for r in range(plan.rows):
+            send[s, :, r, :] = total[r * plan.groups : (r + 1) * plan.groups, s * 128 : (s + 1) * 128]
+
+    pl.semaphore_wait(barrier, plan.count - 1)
+    used = pl.ds(0, plan.rows)
+    copies = []
+    for i, offset in enumerate(offsets):
+        to, source = spread(offset)
+        copy = pltpu.make_async_remote_copy(
+            src_ref=send.at[to[2], to[0] * plan.pens + to[1], used],
+            dst_ref=recv.at[me, used],
+            send_sem=send_sem.at[i],
+            recv_sem=recv_sem.at[i],
+            device_id=to,
+            device_id_type=pl.DeviceIdType.MESH,
+        )
+        copy.start()
+        arrival = pltpu.make_async_remote_copy(
+            src_ref=send.at[to[2], to[0] * plan.pens + to[1], used],
+            dst_ref=recv.at[source, used],
+            send_sem=send_sem.at[i],
+            recv_sem=recv_sem.at[i],
+            device_id=to,
+            device_id_type=pl.DeviceIdType.MESH,
+        )
+        copies.append((copy, arrival))
+    recv[me, 0 : plan.rows] = send[slab, group, 0 : plan.rows]
+
+    keep, bm, ky_n = plan.keep, plan.block, plan.rows_ky
+
+    def signed(index):
+        return jnp.where(index < keep // 2, index, index - keep)
+
+    lane = lax.broadcasted_iota(jnp.int32, (keep, 128), 1)
+    inner_lane = lax.rem(lane, plan.field)
+    low_half = lane < plan.field
+    is_real = lax.rem(lane // bm, 2) == 0
+    kx = signed(lax.rem(lane, bm) + slab * bm)
+    ky = signed(inner_lane // (2 * bm) + group * ky_n)
+    kz = signed(lax.broadcasted_iota(jnp.int32, (keep, 128), 0))
+    limit = -(keep // 2)
+    mask = ((kx != limit) & (ky != limit) & (kz != limit)).astype(jnp.float32)
+    kx, ky, kz = (k.astype(jnp.float32) for k in (kx, ky, kz))
+    inverse = 1.0 / jnp.maximum(kx * kx + ky * ky + kz * kz, 1.0)
+    pair = jnp.where(low_half, kx, ky)
+
+    row = lax.broadcasted_iota(jnp.int32, (plan.field, keep), 0)
+    kz_t = signed(lax.broadcasted_iota(jnp.int32, (plan.field, keep), 1)).astype(jnp.float32)
+    kx_t = signed(lax.rem(row, bm) + slab * bm).astype(jnp.float32)
+    ky_t = signed(row // (2 * bm) + group * ky_n).astype(jnp.float32)
+    visc = 0.5 / (keep // 2) ** 2
+    damp = visc * (kx_t * kx_t + ky_t * ky_t + kz_t * kz_t)
+    loads[5].wait()
+    damped = [damp * modes[c].reshape(plan.field, keep) for c in range(3)]
+    loads[4].wait()
+
+    for _, arrival in copies:
+        arrival.wait_recv()
+    got = split_in_kernel(recv[...].reshape(plan.count * 8, 128))
+    out = split_dot((third[0], third[1]), got)
+    out = [out[i * keep : (i + 1) * keep] for i in range(6)]
+
+    def turn(cos_part, sin_part):
+        ahead = pltpu.roll(sin_part, 128 - bm, 1)
+        behind = pltpu.roll(sin_part, bm, 1)
+        return cos_part + jnp.where(is_real, ahead, -behind)
+
+    both = turn(out[0], out[1])
+    last_cos = jnp.where(low_half, out[2], out[4])
+    last_sin = jnp.where(low_half, out[3], out[5])
+    last = turn(last_cos, last_sin)
+    last = last + pltpu.roll(last, plan.field, 1)
+    dots = pair * both
+    inner = (dots + pltpu.roll(dots, plan.field, 1) + kz * last) * inverse
+    both = jnp.transpose((both - pair * inner) * mask)
+    last = jnp.transpose((last - kz * inner) * mask)
+    shape = (ky_n, 2, bm, keep)
+    out_ref[0] = (both[: plan.field] - damped[0]).reshape(shape)
+    out_ref[1] = (both[plan.field :] - damped[1]).reshape(shape)
+    out_ref[2] = (last[: plan.field] - damped[2]).reshape(shape)
+    for copy, _ in copies:
+        copy.wait_send()
+
+
+def direct(plan, tables, velocity, vorticity, velocity_modes):
+    modes = jnp.transpose(velocity_modes, (0, 2, 3, 4, 1))
+    first, second, third = tables
+    hbm = pl.BlockSpec(memory_space=pl.ANY)
+    out = pl.pallas_call(
+        functools.partial(kernel, plan),
+        out_shape=jax.ShapeDtypeStruct(modes.shape, jnp.float32),
+        in_specs=[hbm] * 6,
+        out_specs=pl.BlockSpec(memory_space=pltpu.VMEM),
+        scratch_shapes=[
+            pltpu.VMEM(velocity.shape, jnp.float32),
+            pltpu.VMEM(vorticity.shape, jnp.float32),
+            pltpu.VMEM(modes.shape, jnp.float32),
+            pltpu.VMEM(first.shape[1:], jnp.bfloat16),
+            pltpu.VMEM(second.shape, jnp.bfloat16),
+            pltpu.VMEM(third.shape, jnp.bfloat16),
+            pltpu.VMEM((plan.slabs, plan.groups, 8, 128), jnp.float32),
+            pltpu.VMEM((plan.count, 8, 128), jnp.float32),
+            pltpu.SemaphoreType.DMA((6,)),
+            pltpu.SemaphoreType.DMA((plan.count - 1,)),
+            pltpu.SemaphoreType.DMA((plan.count - 1,)),
+        ],
+        compiler_params=pltpu.CompilerParams(collective_id=0, has_side_effects=True),
+    )(velocity, vorticity, modes, first, second, third)
+    return jnp.transpose(out, (0, 4, 1, 2, 3))
+
+
 def solution(mesh):
+    sizes = dict(mesh.shape)
+
+    def run(velocity, vorticity, velocity_modes):
+        _, z_rows, y_rows, cells = velocity.shape
+        plan = Plan(sizes, cells, velocity_modes.shape[1], z_rows, y_rows)
+        if not plan.fits():
+            return per_device(velocity, vorticity, velocity_modes)
+        return direct(plan, plan.tables(), velocity, vorticity, velocity_modes)
+
     return jax.shard_map(
-        per_device,
+        run,
         mesh=mesh,
         in_specs=(
             P(None, ("section", "pen"), "slab", None),

time: 32.7 us -> 15.1 us (0.46)
  Pallas kernels: 0 us -> 13.4 us
  starting transfers between devices: 11.6 us -> 0 us
  waiting for transfers between devices: 8.39 us -> 0 us
  matrix products: 4 us -> 0 us
  local copies, waits for them, and re-layouts: 5.12 us -> 1.54 us
  other arithmetic: 3 us -> 0 us
    pallas_call x0 -> x1, Pallas kernels: none -> 13.4 us  [direct(): pl.pallas_call(functools.partial(kernel, plan), out_shape=jax.ShapeDtypeS...]
    all_to_all x2 -> x0, starting transfers between devices: 11.6 us -> none  [the longest x1 8.34 us: per_device(): lax.all_to_all(second_pass, ('section', 'pen'), split_axis=2, concat_axis...]
    all_to_all x2 -> x0, waiting for transfers between devices: 8.39 us -> none  [the longest x1 7.01 us: per_device(): lax.all_to_all(second_pass, ('section', 'pen'), split_axis=2, concat_axis...]
    dot_general x9 -> x0, matrix products: 4 us -> none  [the longest x2 0.96 us: complex_apply(): jnp.einsum(form, cosine, imag_part, precision=highest)]
    unnamed x8 -> x1, local copies, waits for them, and re-layouts: 3.2 us -> 1.54 us
    all_to_all x2 -> x0, other arithmetic: 1.37 us -> none  [the longest x1 0.72 us: per_device(): lax.all_to_all(first_pass, 'slab', split_axis=3, concat_axis=2, tiled=True)]
    sub x4 -> x0, other arithmetic: 1.06 us -> none  [the longest x1 0.88 us: per_device(): velocity[1] * vorticity[2] - velocity[2] * vorticity[1]]
    all_to_all x4 -> x0, local copies, waits for them, and re-layouts: 0.72 us -> none  [the longest x2 0.66 us: per_device(): lax.all_to_all(first_pass, 'slab', split_axis=3, concat_axis=2, tiled=True)]
  transfers between devices with their start and end apart: 2 -> 0, of which waited for: 2 -> 0; matrix products, arithmetic and copies ran while one was open for 1% -> 0% of each run, Pallas kernels for 0% -> 0%
where the time goes in v1:
time: 15.1 us; the launch traced here: 14.9 us
  Pallas kernels  13.4 us (89%)
  local copies, waits for them, and re-layouts  1.54 us (10%)
    pallas_call x1, Pallas kernels, direct(): pl.pallas_call(functools.partial(kernel, plan), out_shape=jax.ShapeDtypeS...  13.4 us
    unnamed x1, local copies, waits for them, and re-layouts  1.54 us

profile of v1, /device:TPU:0, one launch (start us, length us, event | category | flops | bytes accessed | tf_op | source)
XLA Modules:
  0.0 14.9 jit_solution(599612470529894339)
XLA Ops:
  0.0 13.4 %shard_map.64 = f32[3,2,2,16,32]{4,3,2,1,0:T(8,128)} custom-call(f32[3,3,24,48]{3,2,1,0:T(8,128)} %vel_hbm.1, f32[3,3,24,48]{3,2,1,0:T(8,128)} %vort_hbm.1, f32[3,2,2,16,32]{4,3,2,1,0:T(8,128)} %bitcast.3, bf16[2,2,640,216]{3,2,1,0:T(8,128)(2,1)} %constant.6.clone.first_hbm, bf16[2,8,48,256]{3,2,1,0:T(8,128)(2,1)} %constant.7.clone.second_hbm, ...), custom_call_target="tpu_custom_call" | custom-call | tf_op jit(solution)/shard_map/pallas_call | solution.py:361
  13.4 1.5 %copy.8 = f32[3,32,2,2,16]{1,4,3,2,0:T(8,128)} copy(f32[3,32,2,2,16]{1,4,3,2,0:T(8,128)} %bitcast.2) | data formatting | bytes 49152

commit v2 on v1

--- a/solution.py
+++ b/solution.py
@@ -357,10 +357,10 @@
 def direct(plan, tables, velocity, vorticity, velocity_modes):
     modes = jnp.transpose(velocity_modes, (0, 2, 3, 4, 1))
     first, second, third = tables
-    hbm = pl.BlockSpec(memory_space=pl.ANY)
+    hbm = pl.BlockSpec(memory_space=pltpu.HBM)
     out = pl.pallas_call(
         functools.partial(kernel, plan),
-        out_shape=jax.ShapeDtypeStruct(modes.shape, jnp.float32),
+        out_shape=pltpu.VMEM(modes.shape, jnp.float32),
         in_specs=[hbm] * 6,
         out_specs=pl.BlockSpec(memory_space=pltpu.VMEM),
         scratch_shapes=[

time: 15.1 us -> 13.6 us (0.901)
  local copies, waits for them, and re-layouts: 1.54 us -> 0.64 us
  Pallas kernels: 13.4 us -> 12.8 us
    unnamed x1, local copies, waits for them, and re-layouts: 1.54 us -> 0.64 us
    pallas_call x1, Pallas kernels: 13.4 us -> 12.8 us  [direct(): pl.pallas_call(functools.partial(kernel, plan), out_shape=pltpu.VMEM(mode...]
where the time goes in v2:
time: 13.6 us; the launch traced here: 13.4 us
  Pallas kernels  12.8 us (94%)
  local copies, waits for them, and re-layouts  0.64 us (5%)
    pallas_call x1, Pallas kernels, direct(): pl.pallas_call(functools.partial(kernel, plan), out_shape=pltpu.VMEM(mode...  12.8 us
    unnamed x1, local copies, waits for them, and re-layouts  0.64 us

profile of v2, /device:TPU:0, one launch (start us, length us, event | category | flops | bytes accessed | tf_op | source)
XLA Modules:
  0.0 13.4 jit_solution(193414012920066458)
XLA Ops:
  0.0 12.8 %shard_map.64 = f32[3,2,2,16,32]{4,3,2,1,0:T(8,128)S(1)} custom-call(f32[3,3,24,48]{3,2,1,0:T(8,128)} %vel_hbm.1, f32[3,3,24,48]{3,2,1,0:T(8,128)} %vort_hbm.1, f32[3,2,2,16,32]{4,3,2,1,0:T(8,128)} %bitcast.3, bf16[2,2,640,216]{3,2,1,0:T(8,128)(2,1)} %constant.6.clone.first_hbm, bf16[2,8,48,256]{3,2,1,0:T(8,128)(2,1)} %constant.7.clone.second_hbm, ...), custom_call_target="tpu_custom_call" | custom-call | tf_op jit(solution)/shard_map/pallas_call | solution.py:361
  12.8 0.6 %copy.8 = f32[3,32,2,2,16]{1,4,3,2,0:T(8,128)} copy(f32[3,32,2,2,16]{1,4,3,2,0:T(8,128)S(1)} %bitcast.2) | data formatting | bytes 49152

commit v3 on v2

--- a/solution.py
+++ b/solution.py
@@ -184,7 +184,7 @@
                 second[q, 0, :, s, q, 1] = -s_t
                 second[q, 1, :, s, q, 0] = s_t
                 second[q, 1, :, s, q, 1] = c_t
-        second = second.reshape(self.slots * 2, self.cells, self.slabs * 128)
+        second = second.reshape(self.slots, 2 * self.cells, self.slabs * 128)
         third = np.zeros((3, 2, self.keep, g, self.slabs, 8), np.float32)
         for z in range(zl):
             for which, table in enumerate((cos, sin)):
@@ -261,12 +261,12 @@
     cross = split_in_kernel(cross)
     loads[2].wait()
     part = split_dot((first[0], first[1]), cross)
-    part = split_in_kernel(part)
     loads[3].wait()
     size = plan.rows * plan.groups
     total = None
-    for i in range(2 * plan.slots):
-        piece = tuple(p[i * size : (i + 1) * size] for p in part)
+    for i in range(plan.slots):
+        halves = [part[j * size : (j + 1) * size] for j in (2 * i, 2 * i + 1)]
+        piece = split_in_kernel(jnp.concatenate(halves, axis=1))
         term = split_dot(piece, (second[0, i], second[1, i]))
         total = term if total is None else total + term
     for s in range(plan.slabs):

time: 13.6 us -> 13.4 us (0.985)
  Pallas kernels: 12.8 us -> 12.6 us
    pallas_call x1, Pallas kernels: 12.8 us -> 12.6 us  [direct(): pl.pallas_call(functools.partial(kernel, plan), out_shape=pltpu.VMEM(mode...]
where the time goes in v3:
time: 13.4 us; the launch traced here: 13.2 us
  Pallas kernels  12.6 us (94%)
  local copies, waits for them, and re-layouts  0.64 us (5%)
    pallas_call x1, Pallas kernels, direct(): pl.pallas_call(functools.partial(kernel, plan), out_shape=pltpu.VMEM(mode...  12.6 us
    unnamed x1, local copies, waits for them, and re-layouts  0.64 us

profile of v3, /device:TPU:0, one launch (start us, length us, event | category | flops | bytes accessed | tf_op | source)
XLA Modules:
  0.0 13.2 jit_solution(2952458714775515034)
XLA Ops:
  0.0 12.6 %shard_map.64 = f32[3,2,2,16,32]{4,3,2,1,0:T(8,128)S(1)} custom-call(f32[3,3,24,48]{3,2,1,0:T(8,128)} %vel_hbm.1, f32[3,3,24,48]{3,2,1,0:T(8,128)} %vort_hbm.1, f32[3,2,2,16,32]{4,3,2,1,0:T(8,128)} %bitcast.3, bf16[2,2,640,216]{3,2,1,0:T(8,128)(2,1)} %constant.6.clone.first_hbm, bf16[2,4,96,256]{3,2,1,0:T(8,128)(2,1)} %constant.7.clone.second_hbm, ...), custom_call_target="tpu_custom_call" | custom-call | tf_op jit(solution)/shard_map/pallas_call | solution.py:361
  12.6 0.6 %copy.8 = f32[3,32,2,2,16]{1,4,3,2,0:T(8,128)} copy(f32[3,32,2,2,16]{1,4,3,2,0:T(8,128)S(1)} %bitcast.2) | data formatting | bytes 49152
